TPU v7x, 32 devices: a whole 2x2x4 slice. The times are simulated.
32 devices in a mesh: seq: 8 (over z, y), dp: 4 (over x, core).
Axes of the slice: x: 2, y: 2, z: 4, core: 2. Of those that a mesh axis runs over, the one named last changes fastest.
Arguments:
- hidden: bfloat16 [4, 2048, 4608], P('dp', 'seq'), may hold values from -6 to 6
- queries: bfloat16 [4, 2048, 2048], P('dp', 'seq'), may hold values from -64 to 64
- down_weight: bfloat16 [4608, 1024], P('dp'), may hold values from -0.09375 to 0.09375
- up_weight: bfloat16 [2, 512, 1024], P(None, 'dp'), may hold values from -0.25 to 0.25
- lengths: int32 [4], P('dp'), may hold values from 512 to 2048
Outputs:
- latent_cache: bfloat16 [4, 2048, 1024], P('dp', 'seq')
- attended: bfloat16 [4, 2048, 2048], P('dp', 'seq')
All inputs are finite; a program needn't handle non-finite values.
Results may differ from a plain program's by a relative error of at most 0.012.
The roundings to bfloat16 on the way count: a program that leaves them out, or rounds other values in their place, can miss the bound.
Values may be sent and summed in bfloat16 or wider, within the bound.
A program may use at most 128 MiB of HBM per device.

v0:
```python
import functools
import math

import jax
import jax.numpy as jnp
import numpy as np
from jax import lax
from jax.experimental import pallas as pl
from jax.experimental.pallas import tpu as pltpu
from jax.sharding import PartitionSpec as P

HEAD = 128
WINDOW = 4096
MESH = pl.DeviceIdType.MESH

query_scale = 144.0 ** (-0.5)
soft_cap = 50.0
EXP_SCALE = soft_cap * math.log2(math.e)


def angle_tables(rows, blocks):
    half = HEAD // 2
    freqs = 10000.0 ** (-2.0 * np.arange(half, dtype=np.float64) / HEAD)
    freqs = np.concatenate([freqs, freqs])[None, :]
    sign = np.concatenate([-np.ones(half), np.ones(half)])[None, :]
    near = np.arange(rows, dtype=np.float64)[:, None] * freqs
    far = (rows * np.arange(blocks, dtype=np.float64))[:, None] * freqs
    near = np.stack([np.cos(near), sign * np.sin(near)]).astype(np.float32)
    far = np.stack([np.cos(far), sign * np.sin(far)]).astype(np.float32)
    return near, far


def piece_count(quarter):
    for pieces in (6, 4, 2):
        if quarter % (pieces * 16) == 0:
            return pieces
    return 2


def kernel(
    ring, pieces, lengths_ref, hidden_ref, q_ref, down_ref, up_ref, near_ref, far_ref,
    latent_out, attended_out,
    hid, q_raw, qs, wf, up, lat, acc, keys, values, numer, denom, out_buf,
    local_sem, x_send, x_recv, y_send, y_recv, z_send, z_recv, c_send, c_recv, own_send, own_recv,
    up_send, up_recv, chain_send, pair_send, lat_recv, out_sem,
):
    seq = lax.axis_index("seq")
    dp = lax.axis_index("dp")
    rows = lat.shape[1]
    shard = down_ref.shape[0]
    quarter = shard // 4
    piece = quarter // pieces
    split = pieces // 2
    half_rows = rows // 2
    up_rows = up_ref.shape[1]
    groups = qs.shape[0]
    ratio = qs.shape[1] // rows
    key_rank = lat.shape[2] // 2
    total = ring * rows

    side = lax.rem(seq, 2)
    pair = seq + 1 - 2 * side
    level = lax.rem(seq // 2, 2)
    fellow = seq + 2 - 4 * level
    own_part = 2 * side + level
    pair_part = 2 - 2 * side + level
    fellow_part = 2 * side + 1 - level
    diagonal_part = 3 - own_part
    core = lax.rem(dp, 2)
    mate = dp + 1 - 2 * core
    across = lax.rem(dp + 2, 4)
    diagonal = lax.rem(mate + 2, 4)
    has_next = seq + 2 < ring
    has_prev = seq >= 2

    def local(src, dst, sem):
        return pltpu.make_async_copy(src, dst, sem)

    loads = [
        local(down_ref, wf.at[dp], local_sem.at[0]),
        local(hidden_ref.at[0], hid, local_sem.at[1]),
        local(up_ref, up.at[:, pl.ds(pl.multiple_of(dp * up_rows, up_rows), up_rows), :], local_sem.at[2]),
        local(q_ref.at[0], q_raw, local_sem.at[3]),
    ]
    for load in loads:
        load.start()

    barrier = pltpu.get_barrier_semaphore()

    def greet(device):
        pl.semaphore_signal(barrier, inc=1, device_id=device, device_id_type=MESH)

    greet({"seq": seq, "dp": mate})
    greet({"seq": seq, "dp": across})
    greet({"seq": pair, "dp": dp})

    @pl.when(has_next)
    def _():
        greet({"seq": seq + 2, "dp": dp})

    @pl.when(has_prev)
    def _():
        greet({"seq": seq - 2, "dp": dp})

    pl.semaphore_wait(barrier, 3 + has_next.astype(jnp.int32) + has_prev.astype(jnp.int32))

    def remote(src, dst, send, recv, device):
        return pltpu.make_async_remote_copy(
            src_ref=src, dst_ref=dst, send_sem=send, recv_sem=recv, device_id=device, device_id_type=MESH
        )

    to_mate = {"seq": seq, "dp": mate}
    to_across = {"seq": seq, "dp": across}
    to_pair = {"seq": pair, "dp": dp}
    to_fellow = {"seq": fellow, "dp": dp}
    to_next = {"seq": lax.rem(seq + 2, ring), "dp": dp}

    def part(which, index):
        return pl.ds(pl.multiple_of(which * quarter + index * piece, 16), piece)

    def x_copy(index):
        return remote(
            down_ref.at[part(own_part, index)], wf.at[dp, part(own_part, index)],
            x_send.at[index], x_recv.at[index], to_across,
        )

    def y_copy(which, slot):
        view = wf.at[across, part(which, slot % pieces)]
        return remote(view, view, y_send.at[slot], y_recv.at[slot], to_pair)

    def z_copy(which, slot):
        view = wf.at[across, part(which, slot % pieces)]
        return remote(view, view, z_send.at[slot], z_recv.at[slot], to_fellow)

    def c_copy(slot, which, index):
        view = wf.at[across, part(which, index)]
        return remote(view, view, c_send.at[slot, index], c_recv.at[slot, index], to_mate)

    x_copies = [x_copy(i) for i in range(pieces)]
    for copy in x_copies:
        copy.start()
    own_copy = remote(down_ref, wf.at[dp], own_send, own_recv, to_mate)
    own_copy.start()

    def up_view(owner):
        return up.at[:, pl.ds(pl.multiple_of(owner * up_rows, up_rows), up_rows), :]

    up_across = remote(up_ref, up_view(dp), up_send.at[0], up_recv.at[0], to_across)
    up_across.start()
    up_mate = remote(up_ref, up_view(dp), up_send.at[1], up_recv.at[1], to_mate)
    up_mate.start()

    loads[3].wait()
    for g in range(groups):
        for r in range(ratio):
            column = (g * ratio + r) * HEAD
            qs[g, r * rows : (r + 1) * rows, :] = q_raw[:, column : column + HEAD]
    numer[...] = jnp.zeros_like(numer)
    denom[...] = jnp.zeros_like(denom)

    def project(owner):
        columns = pl.ds(pl.multiple_of(owner * shard, 128), shard)
        return jnp.dot(hid[:, columns], wf[owner], preferred_element_type=jnp.float32)

    loads[1].wait()
    loads[0].wait()
    acc[...] = project(dp)

    y_copies = [y_copy(own_part, i) for i in range(pieces)]
    z_copies = [z_copy(own_part, i) for i in range(pieces)]
    relays = [
        y_copy(fellow_part, pieces + i) if i < split else z_copy(pair_part, pieces + i)
        for i in range(pieces)
    ]
    mate_copies = [
        [c_copy(slot, which, i) for i in range(pieces)]
        for slot, which in enumerate((own_part, pair_part, fellow_part, diagonal_part))
    ]

    def pass_on(i):
        y_copies[i].wait_recv()
        if i >= split:
            relays[i].start()
        mate_copies[1][i].start()
        z_copies[i].wait_recv()
        if i < split:
            relays[i].start()
        mate_copies[2][i].start()

    for i in range(pieces):
        x_copies[i].wait_recv()
        y_copies[i].start()
        z_copies[i].start()
        mate_copies[0][i].start()
        if i >= 1:
            pass_on(i - 1)
    pass_on(pieces - 1)
    own_copy.wait_recv()
    acc[...] += project(mate)
    for i in range(pieces):
        relays[i].wait_recv()
        mate_copies[3][i].start()
    acc[...] += project(across)
    for copies in mate_copies:
        for copy in copies:
            copy.wait_recv()
    live_count = lengths_ref[0] - seq * rows
    total_rows = acc[...] + project(diagonal)
    live = lax.broadcasted_iota(jnp.int32, total_rows.shape, 0) < live_count
    lat[seq] = jnp.where(live, total_rows, 0.0).astype(jnp.bfloat16)

    def chain(block, part_index):
        view = lat.at[block, pl.ds(part_index * half_rows, half_rows)]
        return remote(
            view, view, chain_send.at[block, part_index], lat_recv.at[block, part_index], to_next
        )

    def swap(block, part_index):
        view = lat.at[block, pl.ds(part_index * half_rows, half_rows)]
        return remote(
            view, view, pair_send.at[block, part_index], lat_recv.at[block, part_index], to_pair
        )

    @pl.when(has_next)
    def _():
        chain(seq, 0).start()
        chain(seq, 1).start()

    @pl.when(side == 0)
    def _():
        swap(seq, 0).start()
        swap(seq, 1).start()

    latent_copy = local(lat.at[seq], latent_out.at[0], out_sem.at[groups])
    latent_copy.start()

    up_mate.wait_recv()
    up_across.wait_recv()
    up_relay = remote(up_view(across), up_view(across), up_send.at[2], up_recv.at[2], to_mate)
    up_relay.start()
    loads[2].wait()
    up_relay.wait_recv()

    def attend(block, distance, masked):
        latent = lat[block]
        near_cos, near_sin = near_ref[0], near_ref[1]
        far_cos = far_ref[0, pl.ds(block, 1), :]
        far_sin = far_ref[1, pl.ds(block, 1), :]
        cosine = near_cos * far_cos - near_sin * far_sin
        sine = near_sin * far_cos + near_cos * far_sin
        keys_raw = jnp.dot(latent[:, :key_rank], up[0], preferred_element_type=jnp.float32)
        for g in range(groups):
            head = keys_raw[:, g * HEAD : (g + 1) * HEAD]
            turned = head * cosine + pltpu.roll(head, HEAD // 2, 1) * sine
            keys[g] = turned.astype(jnp.bfloat16)
        values_raw = jnp.dot(latent[:, key_rank:], up[1], preferred_element_type=jnp.float32)
        for g in range(groups):
            values[g] = values_raw[:, g * HEAD : (g + 1) * HEAD].astype(jnp.bfloat16)
        if masked:
            shape = (rows, rows)
            gap = (
                lax.broadcasted_iota(jnp.int32, shape, 0)
                - lax.broadcasted_iota(jnp.int32, shape, 1)
                + distance * rows
            )
            allowed = (gap >= 0) & (gap < WINDOW)
            allowed = jnp.concatenate([allowed.astype(jnp.float32)] * ratio, axis=0)
        for g in range(groups):
            raw = lax.dot_general(
                qs[g], keys[g], (((1,), (1,)), ((), ())), preferred_element_type=jnp.float32
            )
            expo = jnp.exp2(EXP_SCALE * jnp.tanh(raw * (query_scale / soft_cap)))
            if masked:
                expo = expo * allowed
            partial = expo[:, :HEAD]
            for column in range(HEAD, rows, HEAD):
                partial = partial + expo[:, column : column + HEAD]
            denom[g] += partial
            numer[g] += jnp.dot(expo.astype(jnp.bfloat16), values[g], preferred_element_type=jnp.float32)

    attend(seq, 0, True)

    def step(k, carry):
        block = seq - k
        odd = lax.rem(k, 2) == 1

        @pl.when(odd & (k + 1 <= seq))
        def _():
            arrived = block - 1
            for h in range(2):
                chain(arrived, h).wait_recv()

                @pl.when(has_next)
                def _():
                    chain(arrived, h).start()

                if h == 0:
                    swap(arrived, h).start()
                else:

                    @pl.when(arrived > 0)
                    def _():
                        swap(arrived, h).start()

        @pl.when(odd)
        def _():
            swap(block, 0).wait_recv()
            swap(block, 1).wait_recv()

            @pl.when((block == 0) & has_next & (side == 1))
            def _():
                chain(block, 1).start()

        if total <= WINDOW:
            attend(block, k, False)
        else:
            edge = (k + 1) * rows > WINDOW

            @pl.when(jnp.logical_not(edge))
            def _():
                attend(block, k, False)

            @pl.when(edge & ((k - 1) * rows < WINDOW))
            def _():
                attend(block, k, True)

        return carry

    lax.fori_loop(1, seq + 1, step, 0)

    live_rows = lax.broadcasted_iota(jnp.int32, (rows, HEAD), 0) < live_count
    width = ratio * HEAD
    for g in range(groups):
        result = numer[g] / jnp.sum(denom[g], axis=1, keepdims=True)
        for r in range(ratio):
            column = g * width + r * HEAD
            piece_out = jnp.where(live_rows, result[r * rows : (r + 1) * rows], 0.0)
            out_buf[:, column : column + HEAD] = piece_out.astype(jnp.bfloat16)
        columns = pl.ds(g * width, width)
        local(out_buf.at[:, columns], attended_out.at[0, :, columns], out_sem.at[g]).start()

    def drain(k, carry):
        block = seq - 2 * k

        @pl.when(has_next)
        def _():
            chain(block, 0).wait_send()
            chain(block, 1).wait_send()

        @pl.when((k > 0) | (side == 0))
        def _():
            swap(block, 0).wait_send()

        @pl.when((side == 1) & (k > 0) | (side == 0) & ((block > 0) | (seq == 0)))
        def _():
            swap(block, 1).wait_send()

        return carry

    lax.fori_loop(0, seq // 2 + 1, drain, 0)

    @pl.when(has_next & (side == 1))
    def _():
        chain(0, 1).wait_send()

    for copy in x_copies + y_copies + z_copies + relays + sum(mate_copies, []) + [own_copy, up_across, up_mate, up_relay]:
        copy.wait_send()
    latent_copy.wait()
    for g in range(groups):
        columns = pl.ds(g * width, width)
        local(out_buf.at[:, columns], attended_out.at[0, :, columns], out_sem.at[g]).wait()


def body(ring, dp_size, hidden, queries, down_weight, up_weight, lengths):
    _, rows, model_dim = hidden.shape
    shard, rank = down_weight.shape
    kv_width = up_weight.shape[2]
    groups = kv_width // HEAD
    q_width = queries.shape[2]
    ratio = q_width // kv_width
    near, far = angle_tables(rows, ring)
    pieces = piece_count(shard // 4)
    any_spec = pl.BlockSpec(memory_space=pl.ANY)
    vmem_spec = pl.BlockSpec(memory_space=pltpu.VMEM)
    f32, bf16, dma = jnp.float32, jnp.bfloat16, pltpu.SemaphoreType.DMA
    return pl.pallas_call(
        functools.partial(kernel, ring, pieces),
        out_shape=(
            jax.ShapeDtypeStruct((1, rows, rank), bf16),
            jax.ShapeDtypeStruct((1, rows, q_width), bf16),
        ),
        in_specs=[pl.BlockSpec(memory_space=pltpu.SMEM)] + [any_spec] * 4 + [vmem_spec] * 2,
        out_specs=(any_spec, any_spec),
        scratch_shapes=[
            pltpu.VMEM((rows, model_dim), bf16),
            pltpu.VMEM((rows, q_width), bf16),
            pltpu.VMEM((groups, ratio * rows, HEAD), bf16),
            pltpu.VMEM((dp_size, shard, rank), bf16),
            pltpu.VMEM((2, dp_size * up_weight.shape[1], kv_width), bf16),
            pltpu.VMEM((ring, rows, rank), bf16),
            pltpu.VMEM((rows, rank), f32),
            pltpu.VMEM((groups, rows, HEAD), bf16),
            pltpu.VMEM((groups, rows, HEAD), bf16),
            pltpu.VMEM((groups, ratio * rows, HEAD), f32),
            pltpu.VMEM((groups, ratio * rows, HEAD), f32),
            pltpu.VMEM((rows, q_width), bf16),
            dma((4,)),
            dma((pieces,)), dma((pieces,)),
            dma((2 * pieces,)), dma((2 * pieces,)),
            dma((2 * pieces,)), dma((2 * pieces,)),
            dma((4, pieces)), dma((4, pieces)),
            dma, dma,
            dma((3,)), dma((3,)),
            dma((ring, 2)), dma((ring, 2)), dma((ring, 2)),
            dma((groups + 1,)),
        ],
        compiler_params=pltpu.CompilerParams(
            collective_id=0, has_side_effects=True, vmem_limit_bytes=60 * 1024 * 1024
        ),
    )(lengths, hidden, queries, down_weight, up_weight, jnp.asarray(near), jnp.asarray(far))


def solution(mesh):
    in_specs = (
        P("dp", "seq", None),
        P("dp", "seq", None),
        P("dp", None),
        P(None, "dp", None),
        P("dp"),
    )
    out_specs = (P("dp", "seq", None), P("dp", "seq", None))
    step = functools.partial(body, mesh.shape["seq"], mesh.shape["dp"])
    return jax.shard_map(step, mesh=mesh, in_specs=in_specs, out_specs=out_specs, check_vma=False)
```

profile of v0, /device:TPU:24, one launch (start us, length us, event | category | flops | bytes accessed | tf_op | source)
XLA Modules:
  0.0 89.3 jit_solution(16270367250245928945)
XLA Ops:
  1.3 83.9 %shard_map.86 = (bf16[1,256,1024]{2,1,0:T(8,128)(2,1)}, bf16[1,256,2048]{2,1,0:T(8,128)(2,1)}) custom-call(s32[1]{0:T(128)S(6)} %copy.11.lengths_ref, bf16[1,256,4608]{2,1,0:T(8,128)(2,1)} %hidden_ref.1, bf16[1,256,2048]{2,1,0:T(8,128)(2,1)} %q_ref.1, bf16[1152,1024]{1,0:T(8,128)(2,1)} %down_ref.1, bf16[2,128,1024]{2,1,0:T(8,128)(2,1)} %up_ref.1, ...), custom_call_target="tpu_custom_call" | custom-call | tf_op jit(solution)/shard_map/pallas_call | solution.py:386
  85.2 1.9 %copy.12 = bf16[1,256,1024]{2,1,0:T(8,128)(2,1)} copy(bf16[1,256,1024]{2,1,0:T(8,128)(2,1)} %get-tuple-element.4) | data formatting | bytes 1048576
  87.0 2.3 %copy.13 = bf16[1,256,2048]{2,1,0:T(8,128)(2,1)} copy(bf16[1,256,2048]{2,1,0:T(8,128)(2,1)} %get-tuple-element.5) | data formatting | bytes 2097152
where the time goes:
time: 89.6 us; the launch traced here: 89.3 us
  Pallas kernels  83.9 us (94%)
  local copies, waits for them, and re-layouts  4.17 us (5%)
  between operations  1.29 us (1%)
    pallas_call x1, Pallas kernels, body(): pl.pallas_call(functools.partial(kernel, ring, pieces), out_shape=(jax.Sh...  83.9 us
    unnamed x2, local copies, waits for them, and re-layouts  4.17 us

commit v1 on v0

v1 whole, which is shorter than its diff:
```python
import functools
import math

import jax
import jax.numpy as jnp
import numpy as np
from jax import lax
from jax.experimental import pallas as pl
from jax.experimental.pallas import tpu as pltpu
from jax.sharding import PartitionSpec as P

HEAD = 128
WINDOW = 4096
MESH = pl.DeviceIdType.MESH

query_scale = 144.0 ** (-0.5)
soft_cap = 50.0
EXP_SCALE = soft_cap * math.log2(math.e)


def angle_tables(rows, blocks):
    half = HEAD // 2
    freqs = 10000.0 ** (-2.0 * np.arange(half, dtype=np.float64) / HEAD)
    freqs = np.concatenate([freqs, freqs])[None, :]
    sign = np.concatenate([-np.ones(half), np.ones(half)])[None, :]
    near = np.arange(rows, dtype=np.float64)[:, None] * freqs
    far = (rows * np.arange(blocks, dtype=np.float64))[:, None] * freqs
    near = np.stack([np.cos(near), sign * np.sin(near)]).astype(np.float32)
    far = np.stack([np.cos(far), sign * np.sin(far)]).astype(np.float32)
    return near, far

UP_PIECES = 2
PARTS = 8
LATE = 5


def kernel(
    ring, lengths_ref, hidden_ref, q_ref, down_ref, up_ref, near_ref, far_ref,
    latent_out, attended_out,
    hid, far_hid, q_raw, qs, wf, up, part_out, part_in, lat, acc, keys, values, numer, denom, out_buf,
    local_sem, own_send, own_recv, h_send, h_recv, p_send, p_recv,
    x_send, x_recv, y_send, y_recv, z_send, z_recv, c_send, c_recv, um_send, um_recv,
    chain_send, pair_send, lat_recv, out_sem,
):
    seq = lax.axis_index("seq")
    dp = lax.axis_index("dp")
    rows = lat.shape[1]
    shard = down_ref.shape[0]
    chip_k = 2 * shard
    part_rows = rows // PARTS
    up_rows = up_ref.shape[1]
    up_half = up_rows // 2
    up_piece = up_half // UP_PIECES
    groups = qs.shape[0]
    ratio = qs.shape[1] // rows
    key_rank = lat.shape[2] // 2
    total = ring * rows

    side = lax.rem(seq, 2)
    pair = seq + 1 - 2 * side
    level = lax.rem(seq // 2, 2)
    fellow = seq + 2 - 4 * level
    core = lax.rem(dp, 2)
    mate = dp + 1 - 2 * core
    across = lax.rem(dp + 2, 4)
    has_next = seq + 2 < ring

    def local(src, dst, sem):
        return pltpu.make_async_copy(src, dst, sem)

    def k_range(owner):
        return pl.ds(pl.multiple_of(owner // 2 * chip_k, 128), chip_k)

    own_weight = pl.ds(pl.multiple_of(core * shard, 128), shard)

    def up_view(owner, kv, half, index):
        start = owner * up_rows + half * up_half + index * up_piece
        return up.at[kv, pl.ds(pl.multiple_of(start, up_piece), up_piece)]

    def up_shard(owner):
        return up.at[:, pl.ds(pl.multiple_of(owner * up_rows, up_rows), up_rows), :]

    loads = [
        local(down_ref, wf.at[own_weight], local_sem.at[0]),
        local(hidden_ref.at[0, :, k_range(dp)], hid, local_sem.at[1]),
        local(up_ref, up_shard(dp), local_sem.at[2]),
        local(q_ref.at[0], q_raw, local_sem.at[3]),
    ]
    for load in loads:
        load.start()

    barrier = pltpu.get_barrier_semaphore()

    def greet(device):
        pl.semaphore_signal(barrier, inc=1, device_id=device, device_id_type=MESH)

    greet({"seq": seq, "dp": mate})
    greet({"seq": seq, "dp": across})
    greet({"seq": pair, "dp": dp})

    neighbours = 3
    for step in (2, 4, -2, -4):
        exists = (seq + step >= 0) & (seq + step < ring)
        neighbours = neighbours + exists.astype(jnp.int32)

        @pl.when(exists)
        def _(step=step):
            greet({"seq": seq + step, "dp": dp})

    pl.semaphore_wait(barrier, neighbours)

    def remote(src, dst, send, recv, device):
        return pltpu.make_async_remote_copy(
            src_ref=src, dst_ref=dst, send_sem=send, recv_sem=recv, device_id=device, device_id_type=MESH
        )

    to_mate = {"seq": seq, "dp": mate}
    to_across = {"seq": seq, "dp": across}
    to_pair = {"seq": pair, "dp": dp}
    to_fellow = {"seq": fellow, "dp": dp}

    def part_span(p):
        return pl.ds(pl.multiple_of(p * part_rows, part_rows), part_rows)

    def hidden_copy(p):
        return remote(
            hidden_ref.at[0, part_span(p), k_range(across)], far_hid.at[part_span(p)],
            h_send.at[p], h_recv.at[p], to_across,
        )

    def partial_copy(p):
        span = part_span(p)
        return remote(part_out.at[span], part_in.at[span], p_send.at[p], p_recv.at[p], to_across)

    hidden_copy(0).start()
    own_copy = remote(down_ref, wf.at[own_weight], own_send, own_recv, to_mate)
    own_copy.start()

    quarters = ((side, level), (1 - side, level), (side, 1 - level), (1 - side, 1 - level))

    def x_copy(i):
        kv, half = quarters[0]
        start = half * up_half + i * up_piece
        src = up_ref.at[kv, pl.ds(pl.multiple_of(start, up_piece), up_piece)]
        return remote(src, up_view(dp, kv, half, i), x_send.at[i], x_recv.at[i], to_across)

    def y_copy(which, slot):
        view = up_view(across, *quarters[which], slot % UP_PIECES)
        return remote(view, view, y_send.at[slot], y_recv.at[slot], to_pair)

    def z_copy(which, slot):
        view = up_view(across, *quarters[which], slot % UP_PIECES)
        return remote(view, view, z_send.at[slot], z_recv.at[slot], to_fellow)

    def c_copy(which, i):
        view = up_view(across, *quarters[which], i)
        return remote(view, view, c_send.at[which, i], c_recv.at[which, i], to_mate)

    x_copies = [x_copy(i) for i in range(UP_PIECES)]
    for copy in x_copies:
        copy.start()
    hidden_copy(1).start()
    up_mate = remote(up_ref, up_shard(dp), um_send, um_recv, to_mate)
    up_mate.start()
    y_copies = [y_copy(0, i) for i in range(UP_PIECES)]
    z_copies = [z_copy(0, i) for i in range(UP_PIECES)]
    relays = [y_copy(2, UP_PIECES), z_copy(1, UP_PIECES + 1)]
    mate_copies = [[c_copy(which, i) for i in range(UP_PIECES)] for which in range(4)]

    loads[3].wait()
    for g in range(groups):
        for r in range(ratio):
            column = (g * ratio + r) * HEAD
            qs[g, r * rows : (r + 1) * rows, :] = q_raw[:, column : column + HEAD]
    numer[...] = jnp.zeros_like(numer)
    denom[...] = jnp.zeros_like(denom)

    live_count = lengths_ref[0] - seq * rows

    def return_partial(p):
        hidden_copy(p).wait_recv()
        product = jnp.dot(far_hid[part_span(p)], wf[...], preferred_element_type=jnp.float32)
        part_out[part_span(p)] = product.astype(jnp.bfloat16)
        partial_copy(p).start()

    def chain(block, p, step):
        view = lat.at[block, part_span(p)]
        target = {"seq": lax.rem(seq + step, ring), "dp": dp}
        return remote(view, view, chain_send.at[step // 2 - 1, block, p], lat_recv.at[block, p], target)

    def swap(block, p):
        view = lat.at[block, part_span(p)]
        return remote(view, view, pair_send.at[block, p], lat_recv.at[block, p], to_pair)

    def climb(block, p, distance, act):
        for step in (2, 4):

            @pl.when((lax.rem(distance, 4) == 0) & (seq + step < ring))
            def _():
                act(chain(block, p, step))

    def cross(block, p, act):
        @pl.when((block == seq) & (side == 0) | (block < seq) & ((p < LATE) | (block > 0)))
        def _():
            act(swap(block, p))

    def start(copy):
        copy.start()

    def wait_send(copy):
        copy.wait_send()

    def finish_part(p):
        partial_copy(p).wait_recv()
        span = part_span(p)
        summed = acc[span] + part_in[span].astype(jnp.float32)
        position = lax.broadcasted_iota(jnp.int32, summed.shape, 0) + p * part_rows
        lat[seq, span] = jnp.where(position < live_count, summed, 0.0).astype(jnp.bfloat16)
        climb(seq, p, 0, start)
        cross(seq, p, start)

    def receive_same(block, p):
        swap(block, p).wait_recv()
        climb(block, p, seq - block, start)
        cross(block, p, start)

    def receive_other(block, p):
        swap(block, p).wait_recv()

        @pl.when((block == 0) & (side == 1) & (p >= LATE))
        def _():
            climb(block, p, seq - 1, start)

    def attend(pieces, size, mode):
        latents, cosines, sines = [], [], []
        for block, start in pieces:
            span = pl.ds(pl.multiple_of(start, size), size)
            latents.append(lat[block, span, :])
            near_cos, near_sin = near_ref[0, span, :], near_ref[1, span, :]
            far_cos = far_ref[0, pl.ds(block, 1), :]
            far_sin = far_ref[1, pl.ds(block, 1), :]
            cosines.append(near_cos * far_cos - near_sin * far_sin)
            sines.append(near_sin * far_cos + near_cos * far_sin)
        latent = jnp.concatenate(latents, axis=0)
        cosine = jnp.concatenate(cosines, axis=0)
        sine = jnp.concatenate(sines, axis=0)
        keys_raw = jnp.dot(latent[:, :key_rank], up[0], preferred_element_type=jnp.float32)
        for g in range(groups):
            head = keys_raw[:, g * HEAD : (g + 1) * HEAD]
            turned = head * cosine + pltpu.roll(head, HEAD // 2, 1) * sine
            keys[g] = turned.astype(jnp.bfloat16)
        values_raw = jnp.dot(latent[:, key_rank:], up[1], preferred_element_type=jnp.float32)
        for g in range(groups):
            values[g] = values_raw[:, g * HEAD : (g + 1) * HEAD].astype(jnp.bfloat16)
        if mode:
            shape = (rows, rows)
            column = lax.broadcasted_iota(jnp.int32, shape, 1)
            offset = jnp.zeros(shape, jnp.int32)
            for n, (block, start) in enumerate(pieces):
                base = (seq - block) * rows - start + n * size
                offset = jnp.where(column >= n * size, base, offset)
            gap = lax.broadcasted_iota(jnp.int32, shape, 0) - column + offset
            allowed = (gap >= 0) & (gap < WINDOW)
            allowed = jnp.concatenate([allowed.astype(jnp.float32)] * ratio, axis=0)
        for g in range(groups):
            raw = lax.dot_general(
                qs[g], keys[g], (((1,), (1,)), ((), ())), preferred_element_type=jnp.float32
            )
            expo = jnp.exp2(EXP_SCALE * jnp.tanh(raw * (query_scale / soft_cap)))
            if mode:
                expo = expo * allowed
            partial = expo[:, :HEAD]
            for column in range(HEAD, rows, HEAD):
                partial = partial + expo[:, column : column + HEAD]
            denom[g] += partial
            numer[g] += jnp.dot(expo.astype(jnp.bfloat16), values[g], preferred_element_type=jnp.float32)

    def attend_unit(u, carry):
        pieces = []
        for n in range(PARTS):
            index = u * PARTS + n
            p = sum((index >= m * seq).astype(jnp.int32) for m in range(1, PARTS))
            pieces.append((seq - 1 - (index - p * seq), p * part_rows))
        attend(pieces, part_rows, total > WINDOW)
        return carry

    loads[0].wait()
    own_copy.wait_recv()
    return_partial(0)
    hidden_copy(2).start()
    loads[1].wait()
    acc[...] = jnp.dot(hid[...], wf[...], preferred_element_type=jnp.float32)
    for i in range(UP_PIECES):
        x_copies[i].wait_recv()
        y_copies[i].start()
        z_copies[i].start()
        mate_copies[0][i].start()

    def spread_up():
        y_copies[0].wait_recv()
        mate_copies[1][0].start()
        z_copies[0].wait_recv()
        relays[0].start()
        mate_copies[2][0].start()
        y_copies[1].wait_recv()
        relays[1].start()
        mate_copies[1][1].start()
        z_copies[1].wait_recv()
        mate_copies[2][1].start()

    def collect_up():
        for i in range(UP_PIECES):
            relays[i].wait_recv()
            mate_copies[3][i].start()
        up_mate.wait_recv()
        loads[2].wait()
        for copies in mate_copies:
            for copy in copies:
                copy.wait_recv()

    latent_copy = local(lat.at[seq], latent_out.at[0], out_sem.at[groups])
    depth = (seq + 1) // 2
    last_slot = PARTS + depth // 2

    def slot(t, done):
        @pl.when(t < PARTS)
        def _():
            finish_part(t)

        @pl.when(t + 1 < PARTS)
        def _():
            return_partial(t + 1)

        @pl.when(t + 3 < PARTS)
        def _():
            hidden_copy(t + 3).start()

        @pl.when(t == 0)
        def _():
            spread_up()

        def visit(j, carry):
            same, other = seq - 2 * j - 2, seq - 2 * j - 1
            p_same, p_other = t - 1 - j // 2, t - 1 - (j + 1) // 2

            @pl.when((same >= 0) & (p_same >= 0) & (p_same < PARTS))
            def _():
                receive_same(same, p_same)

            @pl.when((p_other >= 0) & (p_other < PARTS))
            def _():
                receive_other(other, p_other)

            return carry

        lax.fori_loop(0, depth, visit, 0)

        @pl.when(t == 2)
        def _():
            collect_up()

        @pl.when(t == PARTS)
        def _():
            latent_copy.start()

        @pl.when(t == jnp.where(has_next, last_slot, PARTS))
        def _():
            attend([(seq, 0)], rows, True)

        complete = jnp.clip(t - depth // 2, 0, PARTS) * seq // PARTS
        upto = jnp.where(has_next, 0, jnp.minimum(complete, done + 1))
        upto = jnp.where(t == last_slot, seq, upto)
        lax.fori_loop(done, upto, attend_unit, 0)
        return upto

    lax.fori_loop(0, last_slot + 1, slot, 0)

    live_rows = lax.broadcasted_iota(jnp.int32, (rows, HEAD), 0) < live_count
    width = ratio * HEAD
    for g in range(groups):
        result = numer[g] / jnp.sum(denom[g], axis=1, keepdims=True)
        for r in range(ratio):
            column = g * width + r * HEAD
            piece_out = jnp.where(live_rows, result[r * rows : (r + 1) * rows], 0.0)
            out_buf[:, column : column + HEAD] = piece_out.astype(jnp.bfloat16)
        columns = pl.ds(g * width, width)
        local(out_buf.at[:, columns], attended_out.at[0, :, columns], out_sem.at[g]).start()

    def drain(k, carry):
        block = seq - 2 * k

        def drain_part(p, inner):
            climb(block, p, 2 * k, wait_send)
            cross(block, p, wait_send)
            return inner

        return lax.fori_loop(0, PARTS, drain_part, carry)

    lax.fori_loop(0, seq // 2 + 1, drain, 0)

    def drain_late(p, carry):
        @pl.when(side == 1)
        def _():
            climb(0, p, seq - 1, wait_send)

        return carry

    lax.fori_loop(LATE, PARTS, drain_late, 0)

    for p in range(PARTS):
        hidden_copy(p).wait_send()
        partial_copy(p).wait_send()
    sent = x_copies + y_copies + z_copies + relays + sum(mate_copies, [])
    for copy in sent + [own_copy, up_mate]:
        copy.wait_send()
    latent_copy.wait()
    for g in range(groups):
        columns = pl.ds(g * width, width)
        local(out_buf.at[:, columns], attended_out.at[0, :, columns], out_sem.at[g]).wait()


def body(ring, dp_size, hidden, queries, down_weight, up_weight, lengths):
    _, rows, model_dim = hidden.shape
    shard, rank = down_weight.shape
    kv_width = up_weight.shape[2]
    groups = kv_width // HEAD
    q_width = queries.shape[2]
    ratio = q_width // kv_width
    near, far = angle_tables(rows, ring)
    any_spec = pl.BlockSpec(memory_space=pl.ANY)
    vmem_spec = pl.BlockSpec(memory_space=pltpu.VMEM)
    f32, bf16, dma = jnp.float32, jnp.bfloat16, pltpu.SemaphoreType.DMA
    return pl.pallas_call(
        functools.partial(kernel, ring),
        out_shape=(
            jax.ShapeDtypeStruct((1, rows, rank), bf16),
            jax.ShapeDtypeStruct((1, rows, q_width), bf16),
        ),
        in_specs=[pl.BlockSpec(memory_space=pltpu.SMEM)] + [any_spec] * 4 + [vmem_spec] * 2,
        out_specs=(any_spec, any_spec),
        scratch_shapes=[
            pltpu.VMEM((rows, 2 * shard), bf16),
            pltpu.VMEM((rows, 2 * shard), bf16),
            pltpu.VMEM((rows, q_width), bf16),
            pltpu.VMEM((groups, ratio * rows, HEAD), bf16),
            pltpu.VMEM((2 * shard, rank), bf16),
            pltpu.VMEM((2, dp_size * up_weight.shape[1], kv_width), bf16),
            pltpu.VMEM((rows, rank), bf16),
            pltpu.VMEM((rows, rank), bf16),
            pltpu.VMEM((ring, rows, rank), bf16),
            pltpu.VMEM((rows, rank), f32),
            pltpu.VMEM((groups, rows, HEAD), bf16),
            pltpu.VMEM((groups, rows, HEAD), bf16),
            pltpu.VMEM((groups, ratio * rows, HEAD), f32),
            pltpu.VMEM((groups, ratio * rows, HEAD), f32),
            pltpu.VMEM((rows, q_width), bf16),
            dma((4,)),
            dma, dma,
            dma((PARTS,)), dma((PARTS,)),
            dma((PARTS,)), dma((PARTS,)),
            dma((UP_PIECES,)), dma((UP_PIECES,)),
            dma((2 * UP_PIECES,)), dma((2 * UP_PIECES,)),
            dma((2 * UP_PIECES,)), dma((2 * UP_PIECES,)),
            dma((4, UP_PIECES)), dma((4, UP_PIECES)),
            dma, dma,
            dma((2, ring, PARTS)), dma((ring, PARTS)), dma((ring, PARTS)),
            dma((groups + 1,)),
        ],
        compiler_params=pltpu.CompilerParams(
            collective_id=0, has_side_effects=True, vmem_limit_bytes=60 * 1024 * 1024
        ),
    )(lengths, hidden, queries, down_weight, up_weight, jnp.asarray(near), jnp.asarray(far))


def solution(mesh):
    in_specs = (
        P("dp", "seq", None),
        P("dp", "seq", None),
        P("dp", None),
        P(None, "dp", None),
        P("dp"),
    )
    out_specs = (P("dp", "seq", None), P("dp", "seq", None))
    step = functools.partial(body, mesh.shape["seq"], mesh.shape["dp"])
    return jax.shard_map(step, mesh=mesh, in_specs=in_specs, out_specs=out_specs, check_vma=False)
```

time: 89.6 us -> 81.8 us (0.913)
  Pallas kernels: 83.9 us -> 76.1 us
    pallas_call x1, Pallas kernels: 83.9 us -> 76.1 us  [body(): pl.pallas_call(functools.partial(kernel, ring), out_shape=(jax.ShapeDtype...]
where the time goes in v1:
time: 81.8 us; the launch traced here: 81.6 us
  Pallas kernels  76.1 us (93%)
  local copies, waits for them, and re-layouts  4.17 us (5%)
  between operations  1.29 us (2%)
    pallas_call x1, Pallas kernels, body(): pl.pallas_call(functools.partial(kernel, ring), out_shape=(jax.ShapeDtype...  76.1 us
    unnamed x2, local copies, waits for them, and re-layouts  4.17 us

profile of v1, /device:TPU:24, one launch (start us, length us, event | category | flops | bytes accessed | tf_op | source)
XLA Modules:
  0.0 81.6 jit_solution(9305321863060090826)
XLA Ops:
  1.3 76.1 %shard_map.86 = (bf16[1,256,1024]{2,1,0:T(8,128)(2,1)}, bf16[1,256,2048]{2,1,0:T(8,128)(2,1)}) custom-call(s32[1]{0:T(128)S(6)} %copy.11.lengths_ref, bf16[1,256,4608]{2,1,0:T(8,128)(2,1)} %hidden_ref.1, bf16[1,256,2048]{2,1,0:T(8,128)(2,1)} %q_ref.1, bf16[1152,1024]{1,0:T(8,128)(2,1)} %down_ref.1, bf16[2,128,1024]{2,1,0:T(8,128)(2,1)} %up_ref.1, ...), custom_call_target="tpu_custom_call" | custom-call | tf_op jit(solution)/shard_map/pallas_call | solution.py:433
  77.4 1.9 %copy.12 = bf16[1,256,1024]{2,1,0:T(8,128)(2,1)} copy(bf16[1,256,1024]{2,1,0:T(8,128)(2,1)} %get-tuple-element.4) | data formatting | bytes 1048576
  79.3 2.3 %copy.13 = bf16[1,256,2048]{2,1,0:T(8,128)(2,1)} copy(bf16[1,256,2048]{2,1,0:T(8,128)(2,1)} %get-tuple-element.5) | data formatting | bytes 2097152

commit v2 on v1

--- a/solution.py
+++ b/solution.py
@@ -30,17 +30,20 @@
     return near, far
 
 UP_PIECES = 2
+VMEM_BYTES = 67043328
+SPARE_BYTES = 32768
 PARTS = 8
-LATE = 5
+LATE = 4
+EAGER = 7
 
 
 def kernel(
-    ring, lengths_ref, hidden_ref, q_ref, down_ref, up_ref, near_ref, far_ref,
+    ring, lengths_hbm, hidden_ref, q_ref, down_ref, up_ref, near_hbm, far_hbm,
     latent_out, attended_out,
-    hid, far_hid, q_raw, qs, wf, up, part_out, part_in, lat, acc, keys, values, numer, denom, out_buf,
+    lengths_ref, near_ref, far_ref, hid, far_hid, q_raw, qs, wf, up, part_out, part_in, lat, acc, keys, values, numer, denom,
     local_sem, own_send, own_recv, h_send, h_recv, p_send, p_recv,
     x_send, x_recv, y_send, y_recv, z_send, z_recv, c_send, c_recv, um_send, um_recv,
-    chain_send, pair_send, lat_recv, out_sem,
+    chain_send, pair_send, lat_recv,
 ):
     seq = lax.axis_index("seq")
     dp = lax.axis_index("dp")
@@ -85,6 +88,9 @@
         local(hidden_ref.at[0, :, k_range(dp)], hid, local_sem.at[1]),
         local(up_ref, up_shard(dp), local_sem.at[2]),
         local(q_ref.at[0], q_raw, local_sem.at[3]),
+        local(near_hbm, near_ref, local_sem.at[4]),
+        local(far_hbm, far_ref, local_sem.at[5]),
+        local(lengths_hbm, lengths_ref, local_sem.at[6]),
     ]
     for load in loads:
         load.start()
@@ -167,7 +173,8 @@
     relays = [y_copy(2, UP_PIECES), z_copy(1, UP_PIECES + 1)]
     mate_copies = [[c_copy(which, i) for i in range(UP_PIECES)] for which in range(4)]
 
-    loads[3].wait()
+    for load in loads[3:]:
+        load.wait()
     for g in range(groups):
         for r in range(ratio):
             column = (g * ratio + r) * HEAD
@@ -318,7 +325,6 @@
             for copy in copies:
                 copy.wait_recv()
 
-    latent_copy = local(lat.at[seq], latent_out.at[0], out_sem.at[groups])
     depth = (seq + 1) // 2
     last_slot = PARTS + depth // 2
 
@@ -353,7 +359,12 @@
 
             return carry
 
-        lax.fori_loop(0, depth, visit, 0)
+        near_visits = jnp.minimum(depth, 1)
+        lax.fori_loop(0, near_visits, visit, 0)
+        complete = jnp.clip(t - 1 - depth // 2, 0, PARTS) * seq // PARTS
+        upto = jnp.where(has_next & (t < EAGER), 0, jnp.minimum(complete, done + 1))
+        lax.fori_loop(done, upto, attend_unit, 0)
+        lax.fori_loop(near_visits, depth, visit, 0)
 
         @pl.when(t == 2)
         def _():
@@ -361,19 +372,12 @@
 
         @pl.when(t == PARTS)
         def _():
-            latent_copy.start()
-
-        @pl.when(t == jnp.where(has_next, last_slot, PARTS))
-        def _():
             attend([(seq, 0)], rows, True)
 
-        complete = jnp.clip(t - depth // 2, 0, PARTS) * seq // PARTS
-        upto = jnp.where(has_next, 0, jnp.minimum(complete, done + 1))
-        upto = jnp.where(t == last_slot, seq, upto)
-        lax.fori_loop(done, upto, attend_unit, 0)
         return upto
 
-    lax.fori_loop(0, last_slot + 1, slot, 0)
+    attended_units = lax.fori_loop(0, last_slot + 1, slot, 0)
+    lax.fori_loop(attended_units, seq, attend_unit, 0)
 
     live_rows = lax.broadcasted_iota(jnp.int32, (rows, HEAD), 0) < live_count
     width = ratio * HEAD
@@ -382,9 +386,8 @@
         for r in range(ratio):
             column = g * width + r * HEAD
             piece_out = jnp.where(live_rows, result[r * rows : (r + 1) * rows], 0.0)
-            out_buf[:, column : column + HEAD] = piece_out.astype(jnp.bfloat16)
-        columns = pl.ds(g * width, width)
-        local(out_buf.at[:, columns], attended_out.at[0, :, columns], out_sem.at[g]).start()
+            attended_out[0, :, column : column + HEAD] = piece_out.astype(jnp.bfloat16)
+    latent_out[0] = lat[seq]
 
     def drain(k, carry):
         block = seq - 2 * k
@@ -413,10 +416,17 @@
     sent = x_copies + y_copies + z_copies + relays + sum(mate_copies, [])
     for copy in sent + [own_copy, up_mate]:
         copy.wait_send()
-    latent_copy.wait()
-    for g in range(groups):
-        columns = pl.ds(g * width, width)
-        local(out_buf.at[:, columns], attended_out.at[0, :, columns], out_sem.at[g]).wait()
+
+
+def deliver(latent_ref, attended_ref, latent_out, attended_out, sem):
+    copies = [
+        pltpu.make_async_copy(attended_ref, attended_out, sem.at[0]),
+        pltpu.make_async_copy(latent_ref, latent_out, sem.at[1]),
+    ]
+    for copy in copies:
+        copy.start()
+    for copy in copies:
+        copy.wait()
 
 
 def body(ring, dp_size, hidden, queries, down_weight, up_weight, lengths):
@@ -430,15 +440,18 @@
     any_spec = pl.BlockSpec(memory_space=pl.ANY)
     vmem_spec = pl.BlockSpec(memory_space=pltpu.VMEM)
     f32, bf16, dma = jnp.float32, jnp.bfloat16, pltpu.SemaphoreType.DMA
-    return pl.pallas_call(
+    latent, attended = pl.pallas_call(
         functools.partial(kernel, ring),
         out_shape=(
-            jax.ShapeDtypeStruct((1, rows, rank), bf16),
-            jax.ShapeDtypeStruct((1, rows, q_width), bf16),
+            pltpu.VMEM((1, rows, rank), bf16),
+            pltpu.VMEM((1, rows, q_width), bf16),
         ),
-        in_specs=[pl.BlockSpec(memory_space=pltpu.SMEM)] + [any_spec] * 4 + [vmem_spec] * 2,
-        out_specs=(any_spec, any_spec),
+        in_specs=[pl.BlockSpec(memory_space=pltpu.HBM)] * 7,
+        out_specs=(vmem_spec, vmem_spec),
         scratch_shapes=[
+            pltpu.SMEM(lengths.shape, jnp.int32),
+            pltpu.VMEM(near.shape, f32),
+            pltpu.VMEM(far.shape, f32),
             pltpu.VMEM((rows, 2 * shard), bf16),
             pltpu.VMEM((rows, 2 * shard), bf16),
             pltpu.VMEM((rows, q_width), bf16),
@@ -453,8 +466,7 @@
             pltpu.VMEM((groups, rows, HEAD), bf16),
             pltpu.VMEM((groups, ratio * rows, HEAD), f32),
             pltpu.VMEM((groups, ratio * rows, HEAD), f32),
-            pltpu.VMEM((rows, q_width), bf16),
-            dma((4,)),
+            dma((7,)),
             dma, dma,
             dma((PARTS,)), dma((PARTS,)),
             dma((PARTS,)), dma((PARTS,)),
@@ -464,12 +476,22 @@
             dma((4, UP_PIECES)), dma((4, UP_PIECES)),
             dma, dma,
             dma((2, ring, PARTS)), dma((ring, PARTS)), dma((ring, PARTS)),
-            dma((groups + 1,)),
         ],
         compiler_params=pltpu.CompilerParams(
-            collective_id=0, has_side_effects=True, vmem_limit_bytes=60 * 1024 * 1024
+            collective_id=0, has_side_effects=True, vmem_limit_bytes=VMEM_BYTES - 2 * rows * (rank + q_width) - SPARE_BYTES
         ),
     )(lengths, hidden, queries, down_weight, up_weight, jnp.asarray(near), jnp.asarray(far))
+    return pl.pallas_call(
+        deliver,
+        out_shape=(
+            jax.ShapeDtypeStruct((1, rows, rank), bf16),
+            jax.ShapeDtypeStruct((1, rows, q_width), bf16),
+        ),
+        in_specs=[vmem_spec, vmem_spec],
+        out_specs=(any_spec, any_spec),
+        scratch_shapes=[dma((2,))],
+        compiler_params=pltpu.CompilerParams(vmem_limit_bytes=8 * 1024 * 1024),
+    )(latent, attended)
 
 
 def solution(mesh):

time: 81.8 us -> 77.1 us (0.943)
  local copies, waits for them, and re-layouts: 4.17 us -> 0 us
    unnamed x2 -> x0, local copies, waits for them, and re-layouts: 4.17 us -> none
    pallas_call x1 -> x2, Pallas kernels: 76.1 us -> 75.5 us  [the longest x1 74.3 us: body(): pl.pallas_call(functools.partial(kernel, ring), out_shape=(pltpu.VMEM((1,...]
where the time goes in v2:
time: 77.1 us; the launch traced here: 76.8 us
  Pallas kernels  75.5 us (98%)
  between operations  1.29 us (2%)
    pallas_call x1, Pallas kernels, body(): pl.pallas_call(functools.partial(kernel, ring), out_shape=(pltpu.VMEM((1,...  74.3 us

profile of v2, /device:TPU:24, one launch (start us, length us, event | category | flops | bytes accessed | tf_op | source)
XLA Modules:
  0.0 76.8 jit_solution(974309087350194559)
XLA Ops:
  1.3 74.3 %shard_map.86 = (bf16[1,256,1024]{2,1,0:T(8,128)(2,1)S(1)}, bf16[1,256,2048]{2,1,0:T(8,128)(2,1)S(1)}) custom-call(s32[1]{0:T(128)S(6)} %copy.9.lengths_hbm, bf16[1,256,4608]{2,1,0:T(8,128)(2,1)} %hidden_ref.1, bf16[1,256,2048]{2,1,0:T(8,128)(2,1)} %q_ref.1, bf16[1152,1024]{1,0:T(8,128)(2,1)} %down_ref.1, bf16[2,128,1024]{2,1,0:T(8,128)(2,1)} %up_ref.1, ...), custom_call_target="tpu_custom_call" | custom-call | tf_op jit(solution)/shard_map/pallas_call | solution.py:443
  75.6 1.2 %shard_map.87 = (bf16[1,256,1024]{2,1,0:T(8,128)(2,1)}, bf16[1,256,2048]{2,1,0:T(8,128)(2,1)}) custom-call(bf16[1,256,1024]{2,1,0:T(8,128)(2,1)S(1)} %get-tuple-element.4.latent_ref, bf16[1,256,2048]{2,1,0:T(8,128)(2,1)S(1)} %get-tuple-element.5.attended_ref), custom_call_target="tpu_custom_call" | custom-call | tf_op jit(solution)/shard_map/pallas_call | solution.py:484

commit v3 on v2

--- a/solution.py
+++ b/solution.py
@@ -33,8 +33,8 @@
 VMEM_BYTES = 67043328
 SPARE_BYTES = 32768
 PARTS = 8
-LATE = 4
-EAGER = 7
+LATE = 5
+EAGER = 6
 
 
 def kernel(
@@ -326,45 +326,48 @@
                 copy.wait_recv()
 
     depth = (seq + 1) // 2
-    last_slot = PARTS + depth // 2
+    last_slot = PARTS + depth // 2 + 1
 
     def slot(t, done):
+        @pl.when(t + 1 < PARTS)
+        def _():
+            return_partial(t + 1)
+
+        @pl.when(t + 3 < PARTS)
+        def _():
+            hidden_copy(t + 3).start()
+
         @pl.when(t < PARTS)
         def _():
             finish_part(t)
 
-        @pl.when(t + 1 < PARTS)
-        def _():
-            return_partial(t + 1)
-
-        @pl.when(t + 3 < PARTS)
-        def _():
-            hidden_copy(t + 3).start()
-
         @pl.when(t == 0)
         def _():
             spread_up()
 
-        def visit(j, carry):
-            same, other = seq - 2 * j - 2, seq - 2 * j - 1
-            p_same, p_other = t - 1 - j // 2, t - 1 - (j + 1) // 2
-
-            @pl.when((same >= 0) & (p_same >= 0) & (p_same < PARTS))
+        def visit_same(j, carry):
+            block, p = seq - 2 * j - 2, t - 1 - j // 2
+
+            @pl.when((block >= 0) & (p >= 0) & (p < PARTS))
             def _():
-                receive_same(same, p_same)
-
-            @pl.when((p_other >= 0) & (p_other < PARTS))
+                receive_same(block, p)
+
+            return carry
+
+        def visit_other(j, carry):
+            p = t - 2 - (j + 1) // 2
+
+            @pl.when((p >= 0) & (p < PARTS))
             def _():
-                receive_other(other, p_other)
+                receive_other(seq - 2 * j - 1, p)
 
             return carry
 
-        near_visits = jnp.minimum(depth, 1)
-        lax.fori_loop(0, near_visits, visit, 0)
-        complete = jnp.clip(t - 1 - depth // 2, 0, PARTS) * seq // PARTS
+        lax.fori_loop(0, depth, visit_same, 0)
+        complete = jnp.clip(t - 2 - depth // 2, 0, PARTS) * seq // PARTS
         upto = jnp.where(has_next & (t < EAGER), 0, jnp.minimum(complete, done + 1))
         lax.fori_loop(done, upto, attend_unit, 0)
-        lax.fori_loop(near_visits, depth, visit, 0)
+        lax.fori_loop(0, depth, visit_other, 0)
 
         @pl.when(t == 2)
         def _():

time: 77.1 us -> 74.5 us (0.966)
  the two profiles are of different devices: /device:TPU:24 before, /device:TPU:28 now
where the time goes in v3:
time: 74.5 us; the launch traced here: 74.3 us
  Pallas kernels  73 us (98%)
  between operations  1.29 us (2%)
    pallas_call x1, Pallas kernels, body(): pl.pallas_call(functools.partial(kernel, ring), out_shape=(pltpu.VMEM((1,...  71.9 us

profile of v3, /device:TPU:28, one launch (start us, length us, event | category | flops | bytes accessed | tf_op | source)
XLA Modules:
  0.0 74.3 jit_solution(2541784674054706356)
XLA Ops:
  1.3 71.9 %shard_map.86 = (bf16[1,256,1024]{2,1,0:T(8,128)(2,1)S(1)}, bf16[1,256,2048]{2,1,0:T(8,128)(2,1)S(1)}) custom-call(s32[1]{0:T(128)S(6)} %copy.9.lengths_hbm, bf16[1,256,4608]{2,1,0:T(8,128)(2,1)} %hidden_ref.1, bf16[1,256,2048]{2,1,0:T(8,128)(2,1)} %q_ref.1, bf16[1152,1024]{1,0:T(8,128)(2,1)} %down_ref.1, bf16[2,128,1024]{2,1,0:T(8,128)(2,1)} %up_ref.1, ...), custom_call_target="tpu_custom_call" | custom-call | tf_op jit(solution)/shard_map/pallas_call | solution.py:446
  73.2 1.2 %shard_map.87 = (bf16[1,256,1024]{2,1,0:T(8,128)(2,1)}, bf16[1,256,2048]{2,1,0:T(8,128)(2,1)}) custom-call(bf16[1,256,1024]{2,1,0:T(8,128)(2,1)S(1)} %get-tuple-element.4.latent_ref, bf16[1,256,2048]{2,1,0:T(8,128)(2,1)S(1)} %get-tuple-element.5.attended_ref), custom_call_target="tpu_custom_call" | custom-call | tf_op jit(solution)/shard_map/pallas_call | solution.py:487
